TPU v7x, 256 devices: a whole 4x4x8 slice. The times are simulated.
256 devices in a mesh: owner: 8 (over x, core), rows: 32 (over z, y).
Axes of the slice: x: 4, y: 4, z: 8, core: 2. Of those that a mesh axis runs over, the one named last changes fastest.
Arguments:
- w_down: float32 [16, 6400, 4096], P('owner', None, 'rows'), may hold values from -0.15625 to 0.15625
- avg_down: bfloat16 [16, 6400, 4096], P('owner', None, 'rows'), may hold values from -0.0390625 to 0.0390625
- router_weight: float32 [4096, 16], P('rows', 'owner'), may hold values from -0.09375 to 0.09375
- router_gain: float32 [4096], P('rows'), may hold values from 0.25 to 1.75
Outputs:
- serve_down: bfloat16 [16, 6400, 4096], P('owner', 'rows')
- scale_down: float32 [16, 6400], P('owner', 'rows')
- serve_router: bfloat16 [4096, 16], replicated
All inputs are finite; a program needn't handle non-finite values. Where the computation divides by a largest or mean magnitude, that divisor is 1e-20 or more.
Results may differ from a plain program's by a relative error of at most 0.001.
Values may be sent and summed in bfloat16 or wider, within the bound.
A program may use at most 64 MiB of HBM per device.

v0:
```python
import jax
import jax.numpy as jnp
from jax import lax
from jax.sharding import PartitionSpec as P

D_MODEL = 4096


def copy_for_each(x, axis):
    count = lax.axis_size(axis)
    return lax.all_to_all(jnp.broadcast_to(x[None], (count, *x.shape)), axis, 0, 0, tiled=True)


def over_copies(x, axis):
    everything = copy_for_each(x, axis)
    return jnp.sum(everything, axis=0)


def laid_out(parts, dim):
    shape = list(parts.shape[1:])
    shape[dim] *= parts.shape[0]
    return jnp.moveaxis(parts, 0, dim).reshape(shape)


def collect(x, axis, dim):
    return laid_out(copy_for_each(x, axis), dim)


def per_device(w_down, avg_down, router_weight, router_gain):
    fresh_down = w_down + avg_down.astype(jnp.float32)
    total_down = over_copies(jnp.sum(jnp.abs(fresh_down), axis=2), "rows")
    scale_down = total_down / D_MODEL
    narrow_down = (fresh_down / jnp.expand_dims(scale_down, 2)).astype(jnp.bfloat16)
    serve_down = lax.all_to_all(narrow_down, "rows", split_axis=1, concat_axis=2, tiled=True)
    scale_down = lax.dynamic_slice_in_dim(
        scale_down, lax.axis_index("rows") * serve_down.shape[1], serve_down.shape[1], axis=1
    )
    part_router = (router_weight * router_gain[:, None]).astype(jnp.bfloat16)
    row_router = collect(part_router, "rows", 0)
    serve_router = collect(row_router, "owner", 1)
    return (serve_down, scale_down, serve_router)


def solution(mesh):
    return jax.shard_map(
        per_device,
        mesh=mesh,
        in_specs=(
            P("owner", None, "rows"),
            P("owner", None, "rows"),
            P("rows", "owner"),
            P("rows"),
        ),
        out_specs=(P("owner", "rows", None), P("owner", "rows"), P()),
        check_vma=False,
    )
```

profile of v0, /device:TPU:9, one launch (start us, length us, event | category | flops | bytes accessed | tf_op | source)
XLA Modules:
  0.0 201.1 jit_solution(2779808520759683975)
XLA Ops:
  0.6 0.7 multiply_convert_fusion
  1.3 0.6 broadcast_in_dim.9
  1.9 11.1 %all-to-all-start.2 = ((bf16[32,128,2]{1,2,0:T(2,128)(2,1)}), bf16[32,128,2]{1,2,0:T(2,128)(2,1)S(1)}, u32[]{:S(2)}, u32[]{:S(2)}) async-start(bf16[32,128,2]{1,2,0:T(2,128)(2,1)} %broadcast_in_dim.9), calls=%async_computation.2 | async-start | bytes 32768 | tf_op jit(solution)/shard_map/all_to_all | solution.py:11
  13.1 5.6 %abs_reduce_fusion = f32[2,6400]{1,0:T(2,128)S(1)} fusion(f32[2,6400,128]{2,1,0:T(8,128)} %param.4, bf16[2,6400,128]{2,1,0:T(8,128)(2,1)} %param.5), kind=kLoop, calls=%fused_computation.1 | loop fusion | flops 6540800 | bytes 9881600 | tf_op jit(solution)/shard_map/reduce_sum | solution.py:31
  18.7 0.0 copy-start
  18.7 2.0 all-to-all-done.2
  20.7 0.4 broadcast_in_dim.8
  21.1 46.8 %all_to_all.33 = f32[32,2,6400]{2,1,0:T(2,128)} all-to-all(f32[32,2,6400]{2,1,0:T(2,128)S(1)} %broadcast_in_dim.8), channel_id=1, replica_groups=mesh['owner'=8,'rows'=32] {'rows'}, dimensions={0} | all-to-all | bytes 3276800 | tf_op jit(solution)/shard_map/all_to_all | solution.py:11
  67.9 0.7 broadcast_in_dim.11
  68.6 6.7 %all-to-all-start.3 = ((bf16[8,4096,2]{1,2,0:T(2,128)(2,1)}), bf16[8,4096,2]{1,2,0:T(2,128)(2,1)S(1)}, u32[]{:S(2)}, u32[]{:S(2)}) async-start(bf16[8,4096,2]{1,2,0:T(2,128)(2,1)} %broadcast_in_dim.11), calls=%async_computation.3 | async-start | bytes 262144 | tf_op jit(solution)/shard_map/all_to_all | solution.py:11
  75.4 1.9 reduce_sum.19
  77.3 0.0 copy-done
  77.3 4.7 %divide_convert_fusion = bf16[2,6400,128]{2,1,0:T(8,128)(2,1)S(1)} fusion(f32[2,6400,128]{2,1,0:T(8,128)} %param.4, bf16[2,6400,128]{2,1,0:T(8,128)(2,1)S(1)} %copy-done, f32[2,6400]{1,0:T(2,128)S(1)} %broadcast_multiply_fusion), kind=kLoop, calls=%fused_computation | loop fusion | flops 6553600 | bytes 13158400 | tf_op jit(solution)/shard_map/convert_element_type | solution.py:33
  82.0 27.9 %copy.31 = bf16[2,6400,128]{2,0,1:T(2,128)(2,1)} copy(bf16[2,6400,128]{2,1,0:T(8,128)(2,1)S(1)} %divide_convert_fusion) | data formatting | bytes 6553600 | tf_op jit(solution)/shard_map/convert_element_type | solution.py:33
  109.9 0.0 all-to-all-done.3
  109.9 5.0 %all-to-all-start.1 = ((bf16[2,6400,128]{2,0,1:T(2,128)(2,1)}), bf16[2,6400,128]{2,0,1:T(2,128)(2,1)S(1)}, u32[]{:S(2)}, u32[]{:S(2)}) async-start(bf16[2,6400,128]{2,0,1:T(2,128)(2,1)} %copy.31), calls=%async_computation.1 | async-start | bytes 6553600 | tf_op jit(solution)/shard_map/all_to_all | solution.py:34
  114.9 0.7 reshape.16
  115.7 0.7 constant_dynamic-slice_fusion
  116.3 76.1 %all-to-all-done.1 = bf16[2,6400,128]{2,0,1:T(2,128)(2,1)S(1)} async-done(((bf16[2,6400,128]{2,0,1:T(2,128)(2,1)}), bf16[2,6400,128]{2,0,1:T(2,128)(2,1)S(1)}, u32[]{:S(2)}, u32[]{:S(2)}) %all-to-all-start.1) | async-done | bytes 3276832 | tf_op jit(solution)/shard_map/all_to_all | solution.py:34
  192.4 2.5 %copy.32 = bf16[2,200,32,128]{3,2,1,0:T(8,128)(2,1)} copy(bf16[2,200,32,128]{3,0,1,2:T(2,128)(2,1)S(1)} %bitcast.9) | data formatting | bytes 6553600 | tf_op jit(solution)/shard_map/all_to_all | solution.py:34
  194.9 6.2 %all_to_all.26 = bf16[2,200,4096]{2,1,0:T(8,128)(2,1)} reshape(bf16[2,200,32,128]{3,2,1,0:T(8,128)(2,1)} %copy.32) | data formatting | bytes 6553600 | tf_op jit(solution)/shard_map/all_to_all | solution.py:34
  (1 shorter events, 0.0 us)
Async XLA Ops:
  1.9 18.8 %all-to-all-start.2 = ((bf16[32,128,2]{1,2,0:T(2,128)(2,1)}), bf16[32,128,2]{1,2,0:T(2,128)(2,1)S(1)}, u32[]{:S(2)}, u32[]{:S(2)}) async-start(bf16[32,128,2]{1,2,0:T(2,128)(2,1)} %broadcast_in_dim.9), calls=%async_computation.2 | async-start | bytes 32768 | tf_op jit(solution)/shard_map/all_to_all | solution.py:11
  18.7 58.6 %copy-start = (bf16[2,6400,128]{2,1,0:T(8,128)(2,1)S(1)}, bf16[2,6400,128]{2,1,0:T(8,128)(2,1)}, u32[]{:S(2)}) copy-start(bf16[2,6400,128]{2,1,0:T(8,128)(2,1)} %param.5) | copy-start | bytes 9830404
  68.6 41.3 %all-to-all-start.3 = ((bf16[8,4096,2]{1,2,0:T(2,128)(2,1)}), bf16[8,4096,2]{1,2,0:T(2,128)(2,1)S(1)}, u32[]{:S(2)}, u32[]{:S(2)}) async-start(bf16[8,4096,2]{1,2,0:T(2,128)(2,1)} %broadcast_in_dim.11), calls=%async_computation.3 | async-start | bytes 262144 | tf_op jit(solution)/shard_map/all_to_all | solution.py:11
  109.9 82.5 %all-to-all-start.1 = ((bf16[2,6400,128]{2,0,1:T(2,128)(2,1)}), bf16[2,6400,128]{2,0,1:T(2,128)(2,1)S(1)}, u32[]{:S(2)}, u32[]{:S(2)}) async-start(bf16[2,6400,128]{2,0,1:T(2,128)(2,1)} %copy.31), calls=%async_computation.1 | async-start | bytes 6553600 | tf_op jit(solution)/shard_map/all_to_all | solution.py:34
where the time goes:
time: 202 us; the launch traced here: 201 us
  waiting for transfers between devices  78.1 us (39%)
  blocking collectives  46.8 us (23%)
  local copies, waits for them, and re-layouts  39.7 us (20%)
  starting transfers between devices  22.9 us (11%)
  other arithmetic  12.9 us (6%)
    all_to_all x1, waiting for transfers between devices, per_device(): lax.all_to_all(narrow_down, 'rows', split_axis=1, concat_axis=2, tiled=True)  76.1 us
    all_to_all x1, blocking collectives, copy_for_each(): lax.all_to_all(jnp.broadcast_to(x[None], (count, *x.shape)), axis, 0, 0,...  46.8 us
    convert_element_type x1, local copies, waits for them, and re-layouts, per_device(): (fresh_down / jnp.expand_dims(scale_down, 2)).astype(jnp.bfloat16)  27.9 us
    all_to_all x2, starting transfers between devices, copy_for_each(): lax.all_to_all(jnp.broadcast_to(x[None], (count, *x.shape)), axis, 0, 0,...  17.8 us
    all_to_all x2, local copies, waits for them, and re-layouts, per_device(): lax.all_to_all(narrow_down, 'rows', split_axis=1, concat_axis=2, tiled=True)  8.72 us
    reduce_sum x1, other arithmetic, per_device(): total_down = over_copies(jnp.sum(jnp.abs(fresh_down), axis=2), 'rows')  5.6 us
    all_to_all x1, starting transfers between devices, per_device(): lax.all_to_all(narrow_down, 'rows', split_axis=1, concat_axis=2, tiled=True)  5.01 us
    convert_element_type x1, other arithmetic, per_device(): (fresh_down / jnp.expand_dims(scale_down, 2)).astype(jnp.bfloat16)  4.74 us
  transfers between devices with their start and end apart: 3, of which 2 were waited for; matrix products, arithmetic and copies ran while one was open for 21% of the time, Pallas kernels for 0%

commit v1 on v0

--- a/solution.py
+++ b/solution.py
@@ -31,7 +31,12 @@
     total_down = over_copies(jnp.sum(jnp.abs(fresh_down), axis=2), "rows")
     scale_down = total_down / D_MODEL
     narrow_down = (fresh_down / jnp.expand_dims(scale_down, 2)).astype(jnp.bfloat16)
-    serve_down = lax.all_to_all(narrow_down, "rows", split_axis=1, concat_axis=2, tiled=True)
+    serve_down = jnp.concatenate(
+        lax.all_to_all(
+            jnp.stack(jnp.split(narrow_down, lax.axis_size("rows"), axis=1)), "rows", 0, 0
+        ),
+        axis=2,
+    )
     scale_down = lax.dynamic_slice_in_dim(
         scale_down, lax.axis_index("rows") * serve_down.shape[1], serve_down.shape[1], axis=1
     )

time: 202 us -> 170 us (0.84)
  local copies, waits for them, and re-layouts: 39.7 us -> 7.53 us
    convert_element_type x1 -> x0, local copies, waits for them, and re-layouts: 27.9 us -> none  [per_device(): (fresh_down / jnp.expand_dims(scale_down, 2)).astype(jnp.bfloat16)]
    all_to_all x2 -> x0, local copies, waits for them, and re-layouts: 8.72 us -> none  [per_device(): lax.all_to_all(narrow_down, 'rows', split_axis=1, concat_axis=2, tiled=True)]
    unnamed x2 -> x35, local copies, waits for them, and re-layouts: 0.01 us -> 2.25 us
    reshape x0 -> x1, local copies, waits for them, and re-layouts: none -> 2.14 us  [per_device(): jnp.concatenate(lax.all_to_all(jnp.stack(jnp.split(narrow_down, lax.axis_...]
  transfers between devices with their start and end apart: 3 -> 3, of which waited for: 2 -> 2; matrix products, arithmetic and copies ran while one was open for 21% -> 8% of each run, Pallas kernels for 0% -> 0%
where the time goes in v1:
time: 170 us; the launch traced here: 169 us
  waiting for transfers between devices  78.1 us (46%)
  blocking collectives  46.8 us (28%)
  starting transfers between devices  22.9 us (13%)
  other arithmetic  12.9 us (8%)
  local copies, waits for them, and re-layouts  7.53 us (4%)
    all_to_all x1, waiting for transfers between devices, per_device(): lax.all_to_all(jnp.stack(jnp.split(narrow_down, lax.axis_size('rows'), ax...  76.1 us
    all_to_all x1, blocking collectives, copy_for_each(): lax.all_to_all(jnp.broadcast_to(x[None], (count, *x.shape)), axis, 0, 0,...  46.8 us
    all_to_all x2, starting transfers between devices, copy_for_each(): lax.all_to_all(jnp.broadcast_to(x[None], (count, *x.shape)), axis, 0, 0,...  17.8 us
    reduce_sum x1, other arithmetic, per_device(): total_down = over_copies(jnp.sum(jnp.abs(fresh_down), axis=2), 'rows')  5.6 us
    all_to_all x1, starting transfers between devices, per_device(): lax.all_to_all(jnp.stack(jnp.split(narrow_down, lax.axis_size('rows'), ax...  5.01 us
    convert_element_type x1, other arithmetic, per_device(): (fresh_down / jnp.expand_dims(scale_down, 2)).astype(jnp.bfloat16)  4.74 us
  transfers between devices with their start and end apart: 3, of which 2 were waited for; matrix products, arithmetic and copies ran while one was open for 8% of the time, Pallas kernels for 0%

profile of v1, /device:TPU:9, one launch (start us, length us, event | category | flops | bytes accessed | tf_op | source)
XLA Modules:
  0.0 169.1 jit_solution(14877156339228353876)
XLA Ops:
  0.6 0.7 multiply_convert_fusion
  1.3 0.6 broadcast_in_dim.9
  1.9 11.1 %all-to-all-start.2 = ((bf16[32,128,2]{1,2,0:T(2,128)(2,1)}), bf16[32,128,2]{1,2,0:T(2,128)(2,1)S(1)}, u32[]{:S(2)}, u32[]{:S(2)}) async-start(bf16[32,128,2]{1,2,0:T(2,128)(2,1)} %broadcast_in_dim.9), calls=%async_computation.2 | async-start | bytes 32768 | tf_op jit(solution)/shard_map/all_to_all | solution.py:11
  13.1 5.6 %abs_reduce_fusion = f32[2,6400]{1,0:T(2,128)S(1)} fusion(f32[2,6400,128]{2,1,0:T(8,128)} %param.4, bf16[2,6400,128]{2,1,0:T(8,128)(2,1)} %param.5), kind=kLoop, calls=%fused_computation.1 | loop fusion | flops 6540800 | bytes 9881600 | tf_op jit(solution)/shard_map/reduce_sum | solution.py:31
  18.7 0.0 copy-start
  18.7 2.0 %all-to-all-done.2 = bf16[32,128,2]{1,2,0:T(2,128)(2,1)S(1)} async-done(((bf16[32,128,2]{1,2,0:T(2,128)(2,1)}), bf16[32,128,2]{1,2,0:T(2,128)(2,1)S(1)}, u32[]{:S(2)}, u32[]{:S(2)}) %all-to-all-start.2) | async-done | bytes 16416 | tf_op jit(solution)/shard_map/all_to_all | solution.py:11
  20.7 0.4 broadcast_in_dim.8
  21.1 46.8 %all_to_all.20 = f32[32,2,6400]{2,1,0:T(2,128)} all-to-all(f32[32,2,6400]{2,1,0:T(2,128)S(1)} %broadcast_in_dim.8), channel_id=1, replica_groups=mesh['owner'=8,'rows'=32] {'rows'}, dimensions={0} | all-to-all | bytes 3276800 | tf_op jit(solution)/shard_map/all_to_all | solution.py:11
  67.9 0.7 broadcast_in_dim.11
  68.6 6.7 %all-to-all-start.3 = ((bf16[8,4096,2]{1,2,0:T(2,128)(2,1)}), bf16[8,4096,2]{1,2,0:T(2,128)(2,1)S(1)}, u32[]{:S(2)}, u32[]{:S(2)}) async-start(bf16[8,4096,2]{1,2,0:T(2,128)(2,1)} %broadcast_in_dim.11), calls=%async_computation.3 | async-start | bytes 262144 | tf_op jit(solution)/shard_map/all_to_all | solution.py:11
  75.4 1.9 %reduce_sum.19 = f32[2,6400]{1,0:T(2,128)S(1)} reduce(f32[32,2,6400]{2,1,0:T(2,128)} %all_to_all.20, f32[]{:T(128)} %constant.6.clone.1), dimensions={0}, to_apply=%region_1.0 | reduce | flops 396800 | bytes 1689604 | tf_op jit(solution)/shard_map/reduce_sum | solution.py:16
  77.3 0.0 copy-done
  77.3 4.7 %divide_convert_fusion = bf16[2,6400,128]{2,1,0:T(8,128)(2,1)S(1)} fusion(f32[2,6400,128]{2,1,0:T(8,128)} %param.4, bf16[2,6400,128]{2,1,0:T(8,128)(2,1)S(1)} %copy-done, f32[2,6400]{1,0:T(2,128)S(1)} %broadcast_multiply_fusion), kind=kLoop, calls=%fused_computation | loop fusion | flops 6553600 | bytes 13158400 | tf_op jit(solution)/shard_map/convert_element_type | solution.py:33
  82.8 0.0 copy-start.1
  82.8 1.7 %copy-done.1 = bf16[32,2,200,128]{3,2,1,0:T(8,128)(2,1)} copy-done((bf16[32,2,200,128]{3,2,1,0:T(8,128)(2,1)}, bf16[32,2,200,128]{3,2,1,0:T(8,128)(2,1)S(1)}, u32[]{:S(2)}) %copy-start.1) | copy-done | bytes 3276824
  84.5 0.0 all-to-all-done.3
  84.5 5.0 %all-to-all-start.1 = ((bf16[32,2,200,128]{3,2,1,0:T(8,128)(2,1)}), bf16[32,2,200,128]{3,2,1,0:T(8,128)(2,1)S(1)}, u32[]{:S(2)}, u32[]{:S(2)}) async-start(bf16[32,2,200,128]{3,2,1,0:T(8,128)(2,1)} %copy-done.1), calls=%async_computation.1 | async-start | bytes 6553600 | tf_op jit(solution)/shard_map/all_to_all | solution.py:35
  89.5 0.7 reshape.24
  90.3 0.7 constant_dynamic-slice_fusion
  90.9 76.1 %all-to-all-done.1 = bf16[32,2,200,128]{3,2,1,0:T(8,128)(2,1)S(1)} async-done(((bf16[32,2,200,128]{3,2,1,0:T(8,128)(2,1)}), bf16[32,2,200,128]{3,2,1,0:T(8,128)(2,1)S(1)}, u32[]{:S(2)}, u32[]{:S(2)}) %all-to-all-start.1) | async-done | bytes 3276832 | tf_op jit(solution)/shard_map/all_to_all | solution.py:35
  167.0 2.1 %copy_bitcast_fusion = bf16[2,200,4096]{2,1,0:T(8,128)(2,1)} fusion(bf16[32,2,200,128]{3,2,1,0:T(8,128)(2,1)S(1)} %all-to-all-done.1), kind=kLoop, calls=%fused_computation.3 | loop fusion | bytes 6553600 | tf_op jit(solution)/shard_map/reshape | solution.py:34
  (33 shorter events, 0.6 us)
Async XLA Ops:
  1.9 18.8 %all-to-all-start.2 = ((bf16[32,128,2]{1,2,0:T(2,128)(2,1)}), bf16[32,128,2]{1,2,0:T(2,128)(2,1)S(1)}, u32[]{:S(2)}, u32[]{:S(2)}) async-start(bf16[32,128,2]{1,2,0:T(2,128)(2,1)} %broadcast_in_dim.9), calls=%async_computation.2 | async-start | bytes 32768 | tf_op jit(solution)/shard_map/all_to_all | solution.py:11
  18.7 58.6 %copy-start = (bf16[2,6400,128]{2,1,0:T(8,128)(2,1)S(1)}, bf16[2,6400,128]{2,1,0:T(8,128)(2,1)}, u32[]{:S(2)}) copy-start(bf16[2,6400,128]{2,1,0:T(8,128)(2,1)} %param.5) | copy-start | bytes 9830404
  68.6 15.9 %all-to-all-start.3 = ((bf16[8,4096,2]{1,2,0:T(2,128)(2,1)}), bf16[8,4096,2]{1,2,0:T(2,128)(2,1)S(1)}, u32[]{:S(2)}, u32[]{:S(2)}) async-start(bf16[8,4096,2]{1,2,0:T(2,128)(2,1)} %broadcast_in_dim.11), calls=%async_computation.3 | async-start | bytes 262144 | tf_op jit(solution)/shard_map/all_to_all | solution.py:11
  82.8 1.7 %copy-start.1 = (bf16[32,2,200,128]{3,2,1,0:T(8,128)(2,1)}, bf16[32,2,200,128]{3,2,1,0:T(8,128)(2,1)S(1)}, u32[]{:S(2)}) copy-start(bf16[32,2,200,128]{3,2,1,0:T(8,128)(2,1)S(1)} %fusion) | copy-start | bytes 9830404
  84.5 82.5 %all-to-all-start.1 = ((bf16[32,2,200,128]{3,2,1,0:T(8,128)(2,1)}), bf16[32,2,200,128]{3,2,1,0:T(8,128)(2,1)S(1)}, u32[]{:S(2)}, u32[]{:S(2)}) async-start(bf16[32,2,200,128]{3,2,1,0:T(8,128)(2,1)} %copy-done.1), calls=%async_computation.1 | async-start | bytes 6553600 | tf_op jit(solution)/shard_map/all_to_all | solution.py:35
